TPU v7x, 32 devices: a whole 2x2x4 slice. The times are simulated.
32 devices in a mesh: section: 4 (over x, core), row: 2 (over y), col: 4 (over z).
Axes of the slice: x: 2, y: 2, z: 4, core: 2. Of those that a mesh axis runs over, the one named last changes fastest.
Arguments:
- hidden: bfloat16 [4, 8, 4096], P(None, None, 'col'), may hold values from -6 to 6
- norm_gain: bfloat16 [4, 4096], P('section', 'col'), may hold values from 0.25 to 1.75
- w_qkv: bfloat16 [4, 4096, 6144], P('section', 'col', 'row'), may hold values from -0.09375 to 0.09375
- w_out: bfloat16 [4, 4096, 4096], P('section', 'row', 'col'), may hold values from -0.09375 to 0.09375
- cache_keys: bfloat16 [4, 4, 8, 128, 8, 128], P('section', None, 'col', None, 'row'), may hold values from -240 to 240, as said below
- cache_values: bfloat16 [4, 4, 8, 128, 8, 128], P('section', None, 'col', None, 'row'), may hold values from -6 to 6
- cache_lengths: int32 [4, 8], P(None, 'col'), may hold values from 1 to 127
Outputs:
- layer_outputs: bfloat16 [4, 4, 8, 4096], P('section', None, None, 'col')
Inputs may be any that keep to these rules, and one draw needn't show every extreme that they name: `cache_keys`: cached keys are of order one except that some sequences may carry much larger keys at a few positions.
All inputs are finite; a program needn't handle non-finite values.
Results may differ from a plain program's by a relative error of at most 0.04.
Values may be sent and summed in bfloat16 or wider, within the bound.
A program may use at most 64 MiB of HBM per device.

v0:
```python
import jax
import jax.numpy as jnp
from jax import lax
from jax.sharding import PartitionSpec as P

D = 4096
HEADS = 32
KVH = 8


def from_behind(x, axis, by):
    peers = lax.axis_size(axis)
    pairs = [(i, i + by) for i in range(peers) if 0 <= i + by < peers]
    return lax.ppermute(x, axis, pairs)


def rotate(vectors, positions):
    half_dim = vectors.shape[-1] // 2
    inverse_freq = 500000.0 ** (-jnp.arange(half_dim, dtype=jnp.float32) * 2.0 / vectors.shape[-1])
    angles = positions * inverse_freq
    angles = jnp.concatenate([angles, angles], axis=-1)
    swapped = jnp.concatenate([-vectors[..., half_dim:], vectors[..., :half_dim]], axis=-1)
    return vectors * jnp.cos(angles) + swapped * jnp.sin(angles)


def attend(queries, new_key, new_value, key_block, value_block, length):
    score_scale = 1.0 / jnp.sqrt(jnp.float32(queries.shape[-1]))
    scores = (
        jnp.einsum("bgrd,bjgd->bgrj", queries, key_block, preferred_element_type=jnp.float32)
        * score_scale
    )
    own_score = (
        jnp.einsum("bgrd,bgd->bgr", queries, new_key, preferred_element_type=jnp.float32)
        * score_scale
    )
    visible = jnp.arange(key_block.shape[1])[None, :] < length[:, None]
    scores = jnp.where(visible[:, None, None, :], scores, -jnp.inf)
    row_max = jnp.maximum(jnp.max(scores, axis=-1), own_score)
    cache_exp = jnp.exp(scores - row_max[..., None])
    own_exp = jnp.exp(own_score - row_max)
    total = jnp.sum(cache_exp, axis=-1) + own_exp
    cache_weight = (cache_exp / total[..., None]).astype(jnp.bfloat16)
    own_weight = (own_exp / total).astype(jnp.bfloat16)
    result = jnp.einsum(
        "bgrj,bjgd->bgrd", cache_weight, value_block, preferred_element_type=jnp.float32
    )
    result = (
        result
        + own_weight.astype(jnp.float32)[..., None] * new_value.astype(jnp.float32)[:, :, None, :]
    )
    return result.astype(jnp.bfloat16)


def shards(hidden, norm_gain, w_qkv, w_out, cache_keys, cache_values, cache_lengths):
    section_count = lax.axis_size("section")
    section_at = lax.axis_index("section")
    col_count = lax.axis_size("col")
    micro_count = hidden.shape[0]
    batch_size = hidden.shape[1]
    seq_part = batch_size // col_count
    gain_row = norm_gain[0]
    proj_weight = w_qkv[0]
    out_weight = w_out[0]
    groups = cache_keys.shape[4]
    head_dim = cache_keys.shape[5]
    per_group = HEADS // KVH
    tick_count = micro_count + section_count - 1

    def layer_part(current, key_block, value_block, length):
        h_float = current.astype(jnp.float32)
        scaled = (h_float * gain_row.astype(jnp.float32)).astype(jnp.bfloat16)
        squares = jnp.sum(h_float * h_float, axis=1)
        partial_value = jnp.dot(scaled, proj_weight, preferred_element_type=jnp.float32)
        projected, own_squares = (
            lax.psum_scatter(partial_value, "col", scatter_dimension=0, tiled=True),
            lax.psum_scatter(squares, "col", scatter_dimension=0, tiled=True),
        )
        factor = lax.rsqrt(own_squares / D + 1e-05)
        projected = (projected * factor[:, None]).reshape(seq_part, groups, per_group + 2, head_dim)
        positions = length.astype(jnp.float32)
        queries = rotate(projected[:, :, :per_group], positions[:, None, None, None]).astype(
            jnp.bfloat16
        )
        new_key = rotate(projected[:, :, per_group], positions[:, None, None]).astype(jnp.bfloat16)
        new_value = projected[:, :, per_group + 1].astype(jnp.bfloat16)
        attended = attend(queries, new_key, new_value, key_block, value_block, length)
        attended = attended.reshape(seq_part, groups * per_group * head_dim)
        mixed_rows = jnp.dot(
            lax.all_gather(attended, "col", axis=0, tiled=True),
            out_weight,
            preferred_element_type=jnp.float32,
        )
        summed = lax.psum(mixed_rows, "row")
        return (h_float + summed).astype(jnp.bfloat16)

    def advance(tick_at, loop_state):
        received, collected = loop_state
        micro_at = tick_at - section_at
        active = (micro_at >= 0) & (micro_at < micro_count)
        micro_pick = jnp.clip(micro_at, 0, micro_count - 1)
        entry_rows = lax.dynamic_index_in_dim(
            hidden, jnp.clip(tick_at, 0, micro_count - 1), 0, keepdims=False
        )
        current = jnp.where(section_at == 0, entry_rows, received)
        key_block = lax.dynamic_index_in_dim(cache_keys[0], micro_pick, 0, keepdims=False)
        value_block = lax.dynamic_index_in_dim(cache_values[0], micro_pick, 0, keepdims=False)
        length = lax.dynamic_index_in_dim(cache_lengths, micro_pick, 0, keepdims=False)
        produced = layer_part(current, key_block, value_block, length)
        previous = lax.dynamic_index_in_dim(collected, micro_pick, 0, keepdims=False)
        stored = jnp.where(active, produced, previous)
        collected = lax.dynamic_update_index_in_dim(collected, stored, micro_pick, 0)
        received = from_behind(produced, "section", 1)
        return (received, collected)

    start_rows = jnp.zeros(hidden.shape[1:], jnp.bfloat16)
    start_collected = jnp.zeros(hidden.shape, jnp.bfloat16)
    received, collected = lax.fori_loop(0, tick_count, advance, (start_rows, start_collected))
    return collected[None]


def solution(mesh):
    return jax.shard_map(
        shards,
        mesh=mesh,
        in_specs=(
            P(None, None, "col"),
            P("section", "col"),
            P("section", "col", "row"),
            P("section", "row", "col"),
            P("section", None, "col", None, "row", None),
            P("section", None, "col", None, "row", None),
            P(None, "col"),
        ),
        out_specs=P("section", None, None, "col"),
        check_vma=False,
    )
```

profile of v0, /device:TPU:7, one launch (start us, length us, event | category | flops | bytes accessed | tf_op | source)
XLA Modules:
  0.0 507.4 jit_solution(13046033242243475409)
XLA Ops:
  8.0 492.0 %while.18 = (s32[]{:T(128)}, bf16[8,1024]{1,0:T(8,128)(2,1)S(1)}, bf16[4,8,1024]{2,1,0:T(8,128)(2,1)S(1)}, pred[]{:T(512)}, bf16[4,8,1024]{2,1,0:T(8,128)(2,1)},...) while((s32[]{:T(128)}, bf16[8,1024]{1,0:T(8,128)(2,1)S(1)}, ...), condition=%wide.region_7.8_spmd, body=%wide.region_0.7_spmd.sunk | while | flops 86196720 | bytes 13568984 | solution.py:117
  9.0 4.3 fusion.65
  13.7 9.9 %all-reduce.5 = f32[8]{0:T(128)S(1)} all-reduce(f32[8]{0:T(128)S(1)} %get-tuple-element.477), channel_id=3, replica_groups=mesh['section'=4,'row'=2,'col'=4] {'col'}, use_global_device_ids=true, to_apply=%region_3.3.clone | all-reduce | flops 8 | bytes 64 | tf_op jit(solution)/shard_map/while
  26.1 21.0 %all-reduce.8.cloned.1.call-done = f32[8,3072]{1,0:T(8,128)} async-done(((f32[8,3072]{1,0:T(8,128)}), f32[8,3072]{1,0:T(8,128)}) %all-reduce.8.cloned.1.call-update) | async-done | bytes 98320 | tf_op jit(solution)/shard_map/while
  49.3 10.3 %all-gather.2 = bf16[4,2,2048]{2,1,0:T(2,128)(2,1)S(1)} all-gather(bf16[1,2,2048]{2,1,0:T(2,128)(2,1)S(1)} %reshape.350), channel_id=1, replica_groups=mesh['section'=4,'row'=2,'col'=4] {'col'}, dimensions={0}, use_global_device_ids=true | all-gather | bytes 40960 | tf_op jit(solution)/shard_map/while/body/eval_jaxpr/all_gather | solution.py:89
  59.6 2.8 fusion.77
  62.4 5.4 %psum.16 = f32[8,1024]{1,0:T(8,128)S(1)} all-reduce(f32[8,1024]{1,0:T(8,128)S(1)} %fusion.77), channel_id=1, replica_groups=mesh['section'=4,'row'=2,'col'=4] {'row'}, use_global_device_ids=true, to_apply=%region_6.6 | all-reduce | flops 8192 | bytes 65536 | tf_op jit(solution)/shard_map/while/body/eval_jaxpr/psum | solution.py:93
  69.1 8.9 %collective-permute-done = bf16[8,1024]{1,0:T(8,128)(2,1)S(1)} collective-permute-done((bf16[8,1024]{1,0:T(8,128)(2,1)S(1)}, bf16[8,1024]{1,0:T(8,128)(2,1)S(1)}, u32[]{:S(2)}, u32[]{:S(2)}) %collective-permute-start) | collective-permute-done | bytes 16416 | tf_op jit(solution)/shard_map/while/body/eval_jaxpr/ppermute | solution.py:14
  78.9 4.3 fusion.65
  83.6 8.8 %all-reduce.5 = f32[8]{0:T(128)S(1)} all-reduce(f32[8]{0:T(128)S(1)} %get-tuple-element.477), channel_id=3, replica_groups=mesh['section'=4,'row'=2,'col'=4] {'col'}, use_global_device_ids=true, to_apply=%region_3.3.clone | all-reduce | flops 8 | bytes 64 | tf_op jit(solution)/shard_map/while
  94.9 22.5 %all-reduce.8.cloned.1.call-done = f32[8,3072]{1,0:T(8,128)} async-done(((f32[8,3072]{1,0:T(8,128)}), f32[8,3072]{1,0:T(8,128)}) %all-reduce.8.cloned.1.call-update) | async-done | bytes 98320 | tf_op jit(solution)/shard_map/while
  119.6 10.3 %all-gather.2 = bf16[4,2,2048]{2,1,0:T(2,128)(2,1)S(1)} all-gather(bf16[1,2,2048]{2,1,0:T(2,128)(2,1)S(1)} %reshape.350), channel_id=1, replica_groups=mesh['section'=4,'row'=2,'col'=4] {'col'}, dimensions={0}, use_global_device_ids=true | all-gather | bytes 40960 | tf_op jit(solution)/shard_map/while/body/eval_jaxpr/all_gather | solution.py:89
  129.9 2.8 fusion.77
  132.7 5.4 %psum.16 = f32[8,1024]{1,0:T(8,128)S(1)} all-reduce(f32[8,1024]{1,0:T(8,128)S(1)} %fusion.77), channel_id=1, replica_groups=mesh['section'=4,'row'=2,'col'=4] {'row'}, use_global_device_ids=true, to_apply=%region_6.6 | all-reduce | flops 8192 | bytes 65536 | tf_op jit(solution)/shard_map/while/body/eval_jaxpr/psum | solution.py:93
  139.5 8.9 %collective-permute-done = bf16[8,1024]{1,0:T(8,128)(2,1)S(1)} collective-permute-done((bf16[8,1024]{1,0:T(8,128)(2,1)S(1)}, bf16[8,1024]{1,0:T(8,128)(2,1)S(1)}, u32[]{:S(2)}, u32[]{:S(2)}) %collective-permute-start) | collective-permute-done | bytes 16416 | tf_op jit(solution)/shard_map/while/body/eval_jaxpr/ppermute | solution.py:14
  149.2 4.3 fusion.65
  153.9 8.8 %all-reduce.5 = f32[8]{0:T(128)S(1)} all-reduce(f32[8]{0:T(128)S(1)} %get-tuple-element.477), channel_id=3, replica_groups=mesh['section'=4,'row'=2,'col'=4] {'col'}, use_global_device_ids=true, to_apply=%region_3.3.clone | all-reduce | flops 8 | bytes 64 | tf_op jit(solution)/shard_map/while
  165.2 22.5 %all-reduce.8.cloned.1.call-done = f32[8,3072]{1,0:T(8,128)} async-done(((f32[8,3072]{1,0:T(8,128)}), f32[8,3072]{1,0:T(8,128)}) %all-reduce.8.cloned.1.call-update) | async-done | bytes 98320 | tf_op jit(solution)/shard_map/while
  190.0 10.3 %all-gather.2 = bf16[4,2,2048]{2,1,0:T(2,128)(2,1)S(1)} all-gather(bf16[1,2,2048]{2,1,0:T(2,128)(2,1)S(1)} %reshape.350), channel_id=1, replica_groups=mesh['section'=4,'row'=2,'col'=4] {'col'}, dimensions={0}, use_global_device_ids=true | all-gather | bytes 40960 | tf_op jit(solution)/shard_map/while/body/eval_jaxpr/all_gather | solution.py:89
  200.2 2.8 fusion.77
  203.1 5.4 %psum.16 = f32[8,1024]{1,0:T(8,128)S(1)} all-reduce(f32[8,1024]{1,0:T(8,128)S(1)} %fusion.77), channel_id=1, replica_groups=mesh['section'=4,'row'=2,'col'=4] {'row'}, use_global_device_ids=true, to_apply=%region_6.6 | all-reduce | flops 8192 | bytes 65536 | tf_op jit(solution)/shard_map/while/body/eval_jaxpr/psum | solution.py:93
  209.8 8.9 %collective-permute-done = bf16[8,1024]{1,0:T(8,128)(2,1)S(1)} collective-permute-done((bf16[8,1024]{1,0:T(8,128)(2,1)S(1)}, bf16[8,1024]{1,0:T(8,128)(2,1)S(1)}, u32[]{:S(2)}, u32[]{:S(2)}) %collective-permute-start) | collective-permute-done | bytes 16416 | tf_op jit(solution)/shard_map/while/body/eval_jaxpr/ppermute | solution.py:14
  219.5 4.3 fusion.65
  224.3 8.8 %all-reduce.5 = f32[8]{0:T(128)S(1)} all-reduce(f32[8]{0:T(128)S(1)} %get-tuple-element.477), channel_id=3, replica_groups=mesh['section'=4,'row'=2,'col'=4] {'col'}, use_global_device_ids=true, to_apply=%region_3.3.clone | all-reduce | flops 8 | bytes 64 | tf_op jit(solution)/shard_map/while
  235.5 22.5 %all-reduce.8.cloned.1.call-done = f32[8,3072]{1,0:T(8,128)} async-done(((f32[8,3072]{1,0:T(8,128)}), f32[8,3072]{1,0:T(8,128)}) %all-reduce.8.cloned.1.call-update) | async-done | bytes 98320 | tf_op jit(solution)/shard_map/while
  260.3 10.3 %all-gather.2 = bf16[4,2,2048]{2,1,0:T(2,128)(2,1)S(1)} all-gather(bf16[1,2,2048]{2,1,0:T(2,128)(2,1)S(1)} %reshape.350), channel_id=1, replica_groups=mesh['section'=4,'row'=2,'col'=4] {'col'}, dimensions={0}, use_global_device_ids=true | all-gather | bytes 40960 | tf_op jit(solution)/shard_map/while/body/eval_jaxpr/all_gather | solution.py:89
  270.5 2.8 fusion.77
  273.4 5.4 %psum.16 = f32[8,1024]{1,0:T(8,128)S(1)} all-reduce(f32[8,1024]{1,0:T(8,128)S(1)} %fusion.77), channel_id=1, replica_groups=mesh['section'=4,'row'=2,'col'=4] {'row'}, use_global_device_ids=true, to_apply=%region_6.6 | all-reduce | flops 8192 | bytes 65536 | tf_op jit(solution)/shard_map/while/body/eval_jaxpr/psum | solution.py:93
  280.1 8.9 %collective-permute-done = bf16[8,1024]{1,0:T(8,128)(2,1)S(1)} collective-permute-done((bf16[8,1024]{1,0:T(8,128)(2,1)S(1)}, bf16[8,1024]{1,0:T(8,128)(2,1)S(1)}, u32[]{:S(2)}, u32[]{:S(2)}) %collective-permute-start) | collective-permute-done | bytes 16416 | tf_op jit(solution)/shard_map/while/body/eval_jaxpr/ppermute | solution.py:14
  289.9 4.3 fusion.65
  294.6 8.8 %all-reduce.5 = f32[8]{0:T(128)S(1)} all-reduce(f32[8]{0:T(128)S(1)} %get-tuple-element.477), channel_id=3, replica_groups=mesh['section'=4,'row'=2,'col'=4] {'col'}, use_global_device_ids=true, to_apply=%region_3.3.clone | all-reduce | flops 8 | bytes 64 | tf_op jit(solution)/shard_map/while
  305.9 22.5 %all-reduce.8.cloned.1.call-done = f32[8,3072]{1,0:T(8,128)} async-done(((f32[8,3072]{1,0:T(8,128)}), f32[8,3072]{1,0:T(8,128)}) %all-reduce.8.cloned.1.call-update) | async-done | bytes 98320 | tf_op jit(solution)/shard_map/while
  330.6 10.3 %all-gather.2 = bf16[4,2,2048]{2,1,0:T(2,128)(2,1)S(1)} all-gather(bf16[1,2,2048]{2,1,0:T(2,128)(2,1)S(1)} %reshape.350), channel_id=1, replica_groups=mesh['section'=4,'row'=2,'col'=4] {'col'}, dimensions={0}, use_global_device_ids=true | all-gather | bytes 40960 | tf_op jit(solution)/shard_map/while/body/eval_jaxpr/all_gather | solution.py:89
  340.9 2.8 fusion.77
  343.7 5.4 %psum.16 = f32[8,1024]{1,0:T(8,128)S(1)} all-reduce(f32[8,1024]{1,0:T(8,128)S(1)} %fusion.77), channel_id=1, replica_groups=mesh['section'=4,'row'=2,'col'=4] {'row'}, use_global_device_ids=true, to_apply=%region_6.6 | all-reduce | flops 8192 | bytes 65536 | tf_op jit(solution)/shard_map/while/body/eval_jaxpr/psum | solution.py:93
  350.4 8.9 %collective-permute-done = bf16[8,1024]{1,0:T(8,128)(2,1)S(1)} collective-permute-done((bf16[8,1024]{1,0:T(8,128)(2,1)S(1)}, bf16[8,1024]{1,0:T(8,128)(2,1)S(1)}, u32[]{:S(2)}, u32[]{:S(2)}) %collective-permute-start) | collective-permute-done | bytes 16416 | tf_op jit(solution)/shard_map/while/body/eval_jaxpr/ppermute | solution.py:14
  360.2 4.3 fusion.65
  364.9 8.8 %all-reduce.5 = f32[8]{0:T(128)S(1)} all-reduce(f32[8]{0:T(128)S(1)} %get-tuple-element.477), channel_id=3, replica_groups=mesh['section'=4,'row'=2,'col'=4] {'col'}, use_global_device_ids=true, to_apply=%region_3.3.clone | all-reduce | flops 8 | bytes 64 | tf_op jit(solution)/shard_map/while
  376.2 22.5 %all-reduce.8.cloned.1.call-done = f32[8,3072]{1,0:T(8,128)} async-done(((f32[8,3072]{1,0:T(8,128)}), f32[8,3072]{1,0:T(8,128)}) %all-reduce.8.cloned.1.call-update) | async-done | bytes 98320 | tf_op jit(solution)/shard_map/while
  400.9 10.3 %all-gather.2 = bf16[4,2,2048]{2,1,0:T(2,128)(2,1)S(1)} all-gather(bf16[1,2,2048]{2,1,0:T(2,128)(2,1)S(1)} %reshape.350), channel_id=1, replica_groups=mesh['section'=4,'row'=2,'col'=4] {'col'}, dimensions={0}, use_global_device_ids=true | all-gather | bytes 40960 | tf_op jit(solution)/shard_map/while/body/eval_jaxpr/all_gather | solution.py:89
  414.0 5.4 %psum.16 = f32[8,1024]{1,0:T(8,128)S(1)} all-reduce(f32[8,1024]{1,0:T(8,128)S(1)} %fusion.77), channel_id=1, replica_groups=mesh['section'=4,'row'=2,'col'=4] {'row'}, use_global_device_ids=true, to_apply=%region_6.6 | all-reduce | flops 8192 | bytes 65536 | tf_op jit(solution)/shard_map/while/body/eval_jaxpr/psum | solution.py:93
  420.7 8.9 %collective-permute-done = bf16[8,1024]{1,0:T(8,128)(2,1)S(1)} collective-permute-done((bf16[8,1024]{1,0:T(8,128)(2,1)S(1)}, bf16[8,1024]{1,0:T(8,128)(2,1)S(1)}, u32[]{:S(2)}, u32[]{:S(2)}) %collective-permute-start) | collective-permute-done | bytes 16416 | tf_op jit(solution)/shard_map/while/body/eval_jaxpr/ppermute | solution.py:14
  430.5 4.3 fusion.65
  435.2 8.8 %all-reduce.5 = f32[8]{0:T(128)S(1)} all-reduce(f32[8]{0:T(128)S(1)} %get-tuple-element.477), channel_id=3, replica_groups=mesh['section'=4,'row'=2,'col'=4] {'col'}, use_global_device_ids=true, to_apply=%region_3.3.clone | all-reduce | flops 8 | bytes 64 | tf_op jit(solution)/shard_map/while
  446.5 22.5 %all-reduce.8.cloned.1.call-done = f32[8,3072]{1,0:T(8,128)} async-done(((f32[8,3072]{1,0:T(8,128)}), f32[8,3072]{1,0:T(8,128)}) %all-reduce.8.cloned.1.call-update) | async-done | bytes 98320 | tf_op jit(solution)/shard_map/while
  471.2 10.3 %all-gather.2 = bf16[4,2,2048]{2,1,0:T(2,128)(2,1)S(1)} all-gather(bf16[1,2,2048]{2,1,0:T(2,128)(2,1)S(1)} %reshape.350), channel_id=1, replica_groups=mesh['section'=4,'row'=2,'col'=4] {'col'}, dimensions={0}, use_global_device_ids=true | all-gather | bytes 40960 | tf_op jit(solution)/shard_map/while/body/eval_jaxpr/all_gather | solution.py:89
  484.3 5.4 %psum.16 = f32[8,1024]{1,0:T(8,128)S(1)} all-reduce(f32[8,1024]{1,0:T(8,128)S(1)} %fusion.77), channel_id=1, replica_groups=mesh['section'=4,'row'=2,'col'=4] {'row'}, use_global_device_ids=true, to_apply=%region_6.6 | all-reduce | flops 8192 | bytes 65536 | tf_op jit(solution)/shard_map/while/body/eval_jaxpr/psum | solution.py:93
  491.1 8.9 %collective-permute-done = bf16[8,1024]{1,0:T(8,128)(2,1)S(1)} collective-permute-done((bf16[8,1024]{1,0:T(8,128)(2,1)S(1)}, bf16[8,1024]{1,0:T(8,128)(2,1)S(1)}, u32[]{:S(2)}, u32[]{:S(2)}) %collective-permute-start) | collective-permute-done | bytes 16416 | tf_op jit(solution)/shard_map/while/body/eval_jaxpr/ppermute | solution.py:14
  (239 shorter events, 54.0 us)
Async XLA Ops:
  8.0 15.6 %copy-start.1 = (u32[32]{0:T(128)S(1)}, u32[32]{0:T(128)}, u32[]{:S(2)}) copy-start(u32[32]{0:T(128)} %get-tuple-element.547) | copy-start | bytes 388 | tf_op jit(solution)/shard_map/while
  8.0 39.0 %all-reduce.8.cloned.1.call-start = ((), (), s32[]{:S(2)}) async-start(), calls=%async_computation | async-start | bytes 196608 | tf_op jit(solution)/shard_map/while
  67.8 10.2 %collective-permute-start = (bf16[8,1024]{1,0:T(8,128)(2,1)S(1)}, bf16[8,1024]{1,0:T(8,128)(2,1)S(1)}, u32[]{:S(2)}, u32[]{:S(2)}) collective-permute-start(bf16[8,1024]{1,0:T(8,128)(2,1)S(1)} %get-tuple-element.491), channel_id=1, source_target_pairs={{0,8},{8,16},{16,24},{1,9},{9,17},{17,25},{2,10},{10,18},{18,26},{... | collective-permute-start | bytes 49160 | tf_op jit(solution)/shard_map/while/body/eval_jaxpr/ppermute | solution.py:14
  78.1 14.4 %copy-start.1 = (u32[32]{0:T(128)S(1)}, u32[32]{0:T(128)}, u32[]{:S(2)}) copy-start(u32[32]{0:T(128)} %get-tuple-element.547) | copy-start | bytes 388 | tf_op jit(solution)/shard_map/while
  78.1 39.3 %all-reduce.8.cloned.1.call-start = ((), (), s32[]{:S(2)}) async-start(), calls=%async_computation | async-start | bytes 196608 | tf_op jit(solution)/shard_map/while
  138.1 10.2 %collective-permute-start = (bf16[8,1024]{1,0:T(8,128)(2,1)S(1)}, bf16[8,1024]{1,0:T(8,128)(2,1)S(1)}, u32[]{:S(2)}, u32[]{:S(2)}) collective-permute-start(bf16[8,1024]{1,0:T(8,128)(2,1)S(1)} %get-tuple-element.491), channel_id=1, source_target_pairs={{0,8},{8,16},{16,24},{1,9},{9,17},{17,25},{2,10},{10,18},{18,26},{... | collective-permute-start | bytes 49160 | tf_op jit(solution)/shard_map/while/body/eval_jaxpr/ppermute | solution.py:14
  148.4 14.4 %copy-start.1 = (u32[32]{0:T(128)S(1)}, u32[32]{0:T(128)}, u32[]{:S(2)}) copy-start(u32[32]{0:T(128)} %get-tuple-element.547) | copy-start | bytes 388 | tf_op jit(solution)/shard_map/while
  148.4 39.3 %all-reduce.8.cloned.1.call-start = ((), (), s32[]{:S(2)}) async-start(), calls=%async_computation | async-start | bytes 196608 | tf_op jit(solution)/shard_map/while
  208.5 10.2 %collective-permute-start = (bf16[8,1024]{1,0:T(8,128)(2,1)S(1)}, bf16[8,1024]{1,0:T(8,128)(2,1)S(1)}, u32[]{:S(2)}, u32[]{:S(2)}) collective-permute-start(bf16[8,1024]{1,0:T(8,128)(2,1)S(1)} %get-tuple-element.491), channel_id=1, source_target_pairs={{0,8},{8,16},{16,24},{1,9},{9,17},{17,25},{2,10},{10,18},{18,26},{... | collective-permute-start | bytes 49160 | tf_op jit(solution)/shard_map/while/body/eval_jaxpr/ppermute | solution.py:14
  218.7 14.4 %copy-start.1 = (u32[32]{0:T(128)S(1)}, u32[32]{0:T(128)}, u32[]{:S(2)}) copy-start(u32[32]{0:T(128)} %get-tuple-element.547) | copy-start | bytes 388 | tf_op jit(solution)/shard_map/while
  218.7 39.3 %all-reduce.8.cloned.1.call-start = ((), (), s32[]{:S(2)}) async-start(), calls=%async_computation | async-start | bytes 196608 | tf_op jit(solution)/shard_map/while
  278.8 10.2 %collective-permute-start = (bf16[8,1024]{1,0:T(8,128)(2,1)S(1)}, bf16[8,1024]{1,0:T(8,128)(2,1)S(1)}, u32[]{:S(2)}, u32[]{:S(2)}) collective-permute-start(bf16[8,1024]{1,0:T(8,128)(2,1)S(1)} %get-tuple-element.491), channel_id=1, source_target_pairs={{0,8},{8,16},{16,24},{1,9},{9,17},{17,25},{2,10},{10,18},{18,26},{... | collective-permute-start | bytes 49160 | tf_op jit(solution)/shard_map/while/body/eval_jaxpr/ppermute | solution.py:14
  289.0 14.4 %copy-start.1 = (u32[32]{0:T(128)S(1)}, u32[32]{0:T(128)}, u32[]{:S(2)}) copy-start(u32[32]{0:T(128)} %get-tuple-element.547) | copy-start | bytes 388 | tf_op jit(solution)/shard_map/while
  289.0 39.3 %all-reduce.8.cloned.1.call-start = ((), (), s32[]{:S(2)}) async-start(), calls=%async_computation | async-start | bytes 196608 | tf_op jit(solution)/shard_map/while
  349.1 10.2 %collective-permute-start = (bf16[8,1024]{1,0:T(8,128)(2,1)S(1)}, bf16[8,1024]{1,0:T(8,128)(2,1)S(1)}, u32[]{:S(2)}, u32[]{:S(2)}) collective-permute-start(bf16[8,1024]{1,0:T(8,128)(2,1)S(1)} %get-tuple-element.491), channel_id=1, source_target_pairs={{0,8},{8,16},{16,24},{1,9},{9,17},{17,25},{2,10},{10,18},{18,26},{... | collective-permute-start | bytes 49160 | tf_op jit(solution)/shard_map/while/body/eval_jaxpr/ppermute | solution.py:14
  359.3 14.4 %copy-start.1 = (u32[32]{0:T(128)S(1)}, u32[32]{0:T(128)}, u32[]{:S(2)}) copy-start(u32[32]{0:T(128)} %get-tuple-element.547) | copy-start | bytes 388 | tf_op jit(solution)/shard_map/while
  359.3 39.3 %all-reduce.8.cloned.1.call-start = ((), (), s32[]{:S(2)}) async-start(), calls=%async_computation | async-start | bytes 196608 | tf_op jit(solution)/shard_map/while
  419.4 10.2 %collective-permute-start = (bf16[8,1024]{1,0:T(8,128)(2,1)S(1)}, bf16[8,1024]{1,0:T(8,128)(2,1)S(1)}, u32[]{:S(2)}, u32[]{:S(2)}) collective-permute-start(bf16[8,1024]{1,0:T(8,128)(2,1)S(1)} %get-tuple-element.491), channel_id=1, source_target_pairs={{0,8},{8,16},{16,24},{1,9},{9,17},{17,25},{2,10},{10,18},{18,26},{... | collective-permute-start | bytes 49160 | tf_op jit(solution)/shard_map/while/body/eval_jaxpr/ppermute | solution.py:14
  429.7 14.4 %copy-start.1 = (u32[32]{0:T(128)S(1)}, u32[32]{0:T(128)}, u32[]{:S(2)}) copy-start(u32[32]{0:T(128)} %get-tuple-element.547) | copy-start | bytes 388 | tf_op jit(solution)/shard_map/while
  429.7 39.3 %all-reduce.8.cloned.1.call-start = ((), (), s32[]{:S(2)}) async-start(), calls=%async_computation | async-start | bytes 196608 | tf_op jit(solution)/shard_map/while
  489.7 10.2 %collective-permute-start = (bf16[8,1024]{1,0:T(8,128)(2,1)S(1)}, bf16[8,1024]{1,0:T(8,128)(2,1)S(1)}, u32[]{:S(2)}, u32[]{:S(2)}) collective-permute-start(bf16[8,1024]{1,0:T(8,128)(2,1)S(1)} %get-tuple-element.491), channel_id=1, source_target_pairs={{0,8},{8,16},{16,24},{1,9},{9,17},{17,25},{2,10},{10,18},{18,26},{... | collective-permute-start | bytes 49160 | tf_op jit(solution)/shard_map/while/body/eval_jaxpr/ppermute | solution.py:14
  500.0 0.6 copy-start
Sparse Core Ops, SparseCore 0:
  13.5 33.5 all-reduce.7
  83.4 33.9 all-reduce.7
  153.7 33.9 all-reduce.7
  224.0 33.9 all-reduce.7
  294.4 33.9 all-reduce.7
  364.7 33.9 all-reduce.7
  435.0 33.9 all-reduce.7
where the time goes:
time: 512 us; the launch traced here: 507 us
  waiting for transfers between devices  218 us (43%)
  blocking collectives  172 us (34%)
  matrix products  55 us (11%)
  other arithmetic  19.8 us (4%)
  local copies, waits for them, and re-layouts  14.6 us (3%)
  between operations  13.4 us (3%)
  starting transfers between devices  9.1 us (2%)
    while x14, waiting for transfers between devices  156 us
    all_gather x7, blocking collectives, layer_part(): lax.all_gather(attended, 'col', axis=0, tiled=True)  71.8 us
    while x7, blocking collectives  63 us
    ppermute x7, waiting for transfers between devices, from_behind(): return lax.ppermute(x, axis, pairs)  62.5 us
    psum x7, blocking collectives, layer_part(): summed = lax.psum(mixed_rows, 'row')  37.6 us
    dot_general x7, matrix products, layer_part(): jnp.dot(scaled, proj_weight, preferred_element_type=jnp.float32)  30.4 us
    dot_general x7, matrix products, layer_part(): jnp.dot(lax.all_gather(attended, 'col', axis=0, tiled=True), out_weight,...  19.9 us
  transfers between devices with their start and end apart: 14, of which 14 were waited for; matrix products, arithmetic and copies ran while one was open for 3% of the time, Pallas kernels for 0%

commit v1 on v0

v1 whole, which is shorter than its diff:
```python
import functools
import math

import jax
import jax.numpy as jnp
from jax import lax
from jax.experimental import pallas as pl
from jax.experimental.pallas import tpu as pltpu
from jax.sharding import PartitionSpec as P

D = 4096
HEADS = 32
KVH = 8
MESH = pl.DeviceIdType.MESH


def remainder(values, by):
    if by & (by - 1) == 0:
        return values & (by - 1)
    return lax.rem(values, jnp.full_like(values, by))


def kernel(
    dims,
    hidden,
    gain,
    wq_hbm,
    wo_hbm,
    keys_hbm,
    values_hbm,
    lengths,
    out,
    wq,
    wo,
    keys,
    values,
    state,
    part,
    part_in,
    square,
    square_in,
    q_rows,
    k_rows,
    v_rows,
    a_rows,
    attended,
    mixed,
    arrived,
    load_sem,
    rs_send,
    rs_recv,
    sq_send,
    sq_recv,
    at_send,
    at_recv,
    x_send,
    x_recv,
    y_send,
    y_recv,
):
    sections, row_count, cols = dims
    s = lax.axis_index("section")
    r = lax.axis_index("row")
    c = lax.axis_index("col")
    micro, batch, depth = hidden.shape
    rows = micro * batch
    own = rows // cols
    seq_part = batch // cols
    groups, chunk = wq.shape[0], wq.shape[2]
    head_dim = keys.shape[2]
    per = HEADS // KVH
    heads = groups * per
    spots = keys.shape[1]
    pieces, piece = mixed.shape[1], mixed.shape[3]

    def remote(src, dst, send_sem, recv_sem, device):
        return pltpu.make_async_remote_copy(
            src_ref=src,
            dst_ref=dst,
            send_sem=send_sem,
            recv_sem=recv_sem,
            device_id=device,
            device_id_type=MESH,
        )

    loads = [
        pltpu.make_async_copy(
            wq_hbm.at[:, pl.ds(g * chunk, chunk)], wq.at[g], load_sem.at[g]
        )
        for g in range(groups)
    ]
    load_keys = pltpu.make_async_copy(keys_hbm, keys, load_sem.at[groups])
    load_values = pltpu.make_async_copy(values_hbm, values, load_sem.at[groups + 1])
    load_wo = pltpu.make_async_copy(wo_hbm, wo, load_sem.at[groups + 2])
    for load in loads + [load_keys, load_values, load_wo]:
        load.start()

    barrier = pltpu.get_barrier_semaphore()
    greeted = 0
    for k in range(1, cols):
        pl.semaphore_signal(
            barrier, inc=1, device_id=(s, r, lax.rem(c + k, cols)), device_id_type=MESH
        )
        greeted += 1
    for k in range(1, row_count):
        pl.semaphore_signal(
            barrier, inc=1, device_id=(s, lax.rem(r + k, row_count), c), device_id_type=MESH
        )
        greeted += 1
    for step in (1, sections - 1):
        for other in range(row_count):
            pl.semaphore_signal(
                barrier,
                inc=1,
                device_id=(lax.rem(s + step, sections), other, c),
                device_id_type=MESH,
            )
            greeted += 1

    to_row = lax.broadcasted_iota(jnp.int32, (rows, rows), 0)
    from_row = lax.broadcasted_iota(jnp.int32, (rows, rows), 1)
    order = jnp.zeros((rows, rows), jnp.bool_)
    back = jnp.zeros((rows, rows), jnp.bool_)
    for at in range(cols):
        for m in range(micro):
            first, source = at * own + m * seq_part, m * batch + at * seq_part
            inside = (to_row >= first) & (to_row < first + seq_part)
            order = order | (inside & (to_row - from_row == first - source))
            inside = (from_row >= first) & (from_row < first + seq_part)
            back = back | (inside & (from_row - to_row == first - source))
    order = jnp.where(order, 1.0, 0.0).astype(jnp.bfloat16)
    back = jnp.where(back, 1.0, 0.0).astype(jnp.bfloat16)

    row_at = lax.broadcasted_iota(jnp.int32, (own, head_dim), 0)
    lane = lax.broadcasted_iota(jnp.int32, (own, head_dim), 1)
    position = jnp.zeros((own, head_dim), jnp.float32)
    length_of = []
    for m in range(micro):
        for b in range(seq_part):
            length_of.append(lengths[m, b])
            position = jnp.where(
                row_at == m * seq_part + b, length_of[-1].astype(jnp.float32), position
            )
    half = head_dim // 2
    half_lane = jnp.where(lane < half, lane, lane - half).astype(jnp.float32)
    angles = position * jnp.exp(half_lane * (-2.0 * math.log(500000.0) / head_dim))
    cosine = jnp.cos(angles)
    sine = jnp.sin(angles)
    sine = jnp.where(lane < half, -sine, sine)

    def rotate(vectors):
        return vectors * cosine + pltpu.roll(vectors, half, 1) * sine

    head_at = lax.broadcasted_iota(jnp.int32, (heads, spots), 0)
    spot_at = lax.broadcasted_iota(jnp.int32, (heads, spots), 1)
    head_group = jnp.zeros((heads, spots), jnp.int32)
    for g in range(1, groups):
        head_group = head_group + jnp.where(head_at >= g * per, 1, 0)
    same_group = remainder(spot_at, groups) == head_group

    pl.semaphore_wait(barrier, greeted)

    @pl.when(s == 0)
    def _():
        entry = hidden[...].astype(jnp.float32).reshape(rows, depth).astype(jnp.bfloat16)
        state[...] = jnp.dot(order, entry, preferred_element_type=jnp.float32)

    @pl.when(s > 0)
    def _():
        for n in range(pieces):
            for other in range(row_count):
                remote(
                    mixed.at[0, n],
                    arrived.at[other, n],
                    x_send.at[n, 0],
                    x_recv.at[n, other],
                    (s, r, c),
                ).wait_recv()
            total = arrived[0, n]
            for other in range(1, row_count):
                total = total + arrived[other, n]
            state[:, n * piece : (n + 1) * piece] = total.astype(jnp.bfloat16).astype(jnp.float32)

    current = state[...]
    squares = jnp.sum(current * current, axis=1, keepdims=True)
    square[...] = jnp.broadcast_to(squares, (rows, head_dim)).reshape(cols, own, head_dim)
    copies = []
    for k in range(1, cols):
        peer = lax.rem(c + k, cols)
        copies.append(
            remote(
                square.at[peer],
                square_in.at[k - 1],
                sq_send.at[k - 1],
                sq_recv.at[k - 1],
                (s, r, peer),
            )
        )
        copies[-1].start()
    square_copies = copies[:]
    scaled = (current * gain[...].astype(jnp.float32)).astype(jnp.bfloat16)
    part_copies = []
    for g in range(groups):
        loads[g].wait()
        product = jnp.dot(scaled, wq[g], preferred_element_type=jnp.float32)
        part[g] = product.reshape(cols, own, chunk)
        started = []
        for k in range(1, cols):
            peer = lax.rem(c + k, cols)
            started.append(
                remote(
                    part.at[g, peer],
                    part_in.at[g, k - 1],
                    rs_send.at[g, k - 1],
                    rs_recv.at[g, k - 1],
                    (s, r, peer),
                )
            )
            started[-1].start()
        part_copies.append(started)
        copies = copies + started

    for copy in square_copies:
        copy.wait_recv()
    total = square[c]
    for k in range(1, cols):
        total = total + square_in[k - 1]
    factor = lax.rsqrt(total / D + 1e-05)
    for g in range(groups):
        for copy in part_copies[g]:
            copy.wait_recv()
        total = part[g, c]
        for k in range(1, cols):
            total = total + part_in[g, k - 1]
        cut = [total[:, i * head_dim : (i + 1) * head_dim] * factor for i in range(per + 2)]
        new_key = rotate(cut[per]).astype(jnp.bfloat16).astype(jnp.float32)
        new_value = cut[per + 1].astype(jnp.bfloat16).astype(jnp.float32)
        for i in range(per):
            at = pl.ds((g * per + i) * own, own)
            q_rows[at, :] = rotate(cut[i])
            k_rows[at, :] = new_key
            v_rows[at, :] = new_value
    load_keys.wait()
    load_values.wait()
    scale = 1.0 / math.sqrt(head_dim)
    seqs = range(own)
    taken = [pl.ds(i, heads, stride=own) for i in seqs]
    queries = [q_rows[taken[i], :].astype(jnp.bfloat16) for i in seqs]
    scores = [
        lax.dot_general(
            queries[i], keys[i], (((1,), (1,)), ((), ())), preferred_element_type=jnp.float32
        )
        * scale
        for i in seqs
    ]
    own_scores = [
        jnp.sum(queries[i].astype(jnp.float32) * k_rows[taken[i], :], axis=1, keepdims=True) * scale
        for i in seqs
    ]
    weights, own_weights = [], []
    for i in seqs:
        visible = same_group & (spot_at < length_of[i] * groups)
        masked = jnp.where(visible, scores[i], -jnp.inf)
        row_max = jnp.maximum(jnp.max(masked, axis=1, keepdims=True), own_scores[i])
        cache_exp = jnp.exp(masked - row_max)
        own_exp = jnp.exp(own_scores[i] - row_max)
        total = jnp.sum(cache_exp, axis=1, keepdims=True) + own_exp
        weights.append((cache_exp / total).astype(jnp.bfloat16))
        own_weights.append((own_exp / total).astype(jnp.bfloat16).astype(jnp.float32))
    for i in seqs:
        result = jnp.dot(weights[i], values[i], preferred_element_type=jnp.float32)
        a_rows[taken[i], :] = result + own_weights[i] * v_rows[taken[i], :]
    for h in range(heads):
        attended[c, :, h * head_dim : (h + 1) * head_dim] = a_rows[
            h * own : (h + 1) * own, :
        ].astype(jnp.bfloat16)
    started = []
    for k in range(1, cols):
        peer = lax.rem(c + k, cols)
        started.append(
            remote(
                attended.at[c],
                attended.at[c],
                at_send.at[k - 1],
                at_recv.at[k - 1],
                (s, r, peer),
            )
        )
        started[-1].start()
    copies = copies + started
    load_wo.wait()
    for copy in started:
        copy.wait_recv()

    everyone = (
        attended[...].astype(jnp.float32).reshape(rows, heads * head_dim).astype(jnp.bfloat16)
    )

    def onward(n, other):
        return remote(
            mixed.at[r, n],
            arrived.at[r, n],
            x_send.at[n, other],
            x_recv.at[n, r],
            (lax.rem(s + 1, sections), other, c),
        )

    sideways = []
    for n in range(pieces):
        at = slice(n * piece, (n + 1) * piece)
        product = jnp.dot(everyone, wo[:, at], preferred_element_type=jnp.float32)
        mixed[r, n] = product + jnp.where(r == 0, state[:, at], 0.0)

        @pl.when(s < sections - 1)
        def _():
            for other in range(row_count):
                onward(n, other).start()

    for n in range(pieces):
        for k in range(1, row_count):
            peer = lax.rem(r + k, row_count)
            sideways.append(
                remote(
                    mixed.at[r, n],
                    mixed.at[r, n],
                    y_send.at[n, k - 1],
                    y_recv.at[n, k - 1],
                    (s, peer, c),
                )
            )
            sideways[-1].start()
    for copy in sideways:
        copy.wait_recv()
    for n in range(pieces):
        total = mixed[0, n]
        for other in range(1, row_count):
            total = total + mixed[other, n]
        final = jnp.dot(back, total.astype(jnp.bfloat16), preferred_element_type=jnp.float32)
        out[:, :, n * piece : (n + 1) * piece] = final.reshape(micro, batch, piece).astype(
            jnp.bfloat16
        )

    for copy in copies + sideways:
        copy.wait_send()

    @pl.when(s < sections - 1)
    def _():
        for n in range(pieces):
            for other in range(row_count):
                onward(n, other).wait_send()


def shards(hidden, norm_gain, w_qkv, w_out, cache_keys, cache_values, cache_lengths):
    sections, row_count, cols = (lax.axis_size(a) for a in ("section", "row", "col"))
    micro, batch, depth = hidden.shape
    rows = micro * batch
    own = rows // cols
    seqs, spots, groups, head_dim = own, cache_keys.shape[3], *cache_keys.shape[4:]
    per = HEADS // KVH
    heads = groups * per
    chunk = (per + 2) * head_dim
    piece = min(256, w_out.shape[2])
    pieces = w_out.shape[2] // piece
    keys = cache_keys.reshape(seqs, spots * groups, head_dim)
    values = cache_values.reshape(seqs, spots * groups, head_dim)
    vmem = pl.BlockSpec(memory_space=pltpu.VMEM)
    hbm = pl.BlockSpec(memory_space=pl.ANY)
    dma = pltpu.SemaphoreType.DMA
    f32, bf16 = jnp.float32, jnp.bfloat16
    return pl.pallas_call(
        functools.partial(kernel, (sections, row_count, cols)),
        out_shape=jax.ShapeDtypeStruct((micro, batch, depth), bf16),
        in_specs=[vmem, vmem, hbm, hbm, hbm, hbm, pl.BlockSpec(memory_space=pltpu.SMEM)],
        out_specs=vmem,
        scratch_shapes=[
            pltpu.VMEM((groups, depth, chunk), bf16),
            pltpu.VMEM(w_out.shape[1:], bf16),
            pltpu.VMEM(keys.shape, bf16),
            pltpu.VMEM(values.shape, bf16),
            pltpu.VMEM((rows, depth), f32),
            pltpu.VMEM((groups, cols, own, chunk), f32),
            pltpu.VMEM((groups, cols - 1, own, chunk), f32),
            pltpu.VMEM((cols, own, head_dim), f32),
            pltpu.VMEM((cols - 1, own, head_dim), f32),
            pltpu.VMEM((heads * own, head_dim), f32),
            pltpu.VMEM((heads * own, head_dim), f32),
            pltpu.VMEM((heads * own, head_dim), f32),
            pltpu.VMEM((heads * own, head_dim), f32),
            pltpu.VMEM((cols, own, heads * head_dim), bf16),
            pltpu.VMEM((row_count, pieces, rows, piece), f32),
            pltpu.VMEM((row_count, pieces, rows, piece), f32),
            dma((groups + 3,)),
            dma((groups, cols - 1)),
            dma((groups, cols - 1)),
            dma((cols - 1,)),
            dma((cols - 1,)),
            dma((cols - 1,)),
            dma((cols - 1,)),
            dma((pieces, row_count)),
            dma((pieces, row_count)),
            dma((pieces, row_count - 1)),
            dma((pieces, row_count - 1)),
        ],
        compiler_params=pltpu.CompilerParams(collective_id=0, has_side_effects=True),
    )(hidden, norm_gain, w_qkv[0], w_out[0], keys, values, cache_lengths)[None]


def solution(mesh):
    return jax.shard_map(
        shards,
        mesh=mesh,
        in_specs=(
            P(None, None, "col"),
            P("section", "col"),
            P("section", "col", "row"),
            P("section", "row", "col"),
            P("section", None, "col", None, "row", None),
            P("section", None, "col", None, "row", None),
            P(None, "col"),
        ),
        out_specs=P("section", None, None, "col"),
        check_vma=False,
    )
```

time: 512 us -> 72.9 us (0.14)
  waiting for transfers between devices: 218 us -> 0 us
  blocking collectives: 172 us -> 0 us
  Pallas kernels: 0 us -> 69.9 us
  matrix products: 55 us -> 0 us
  other arithmetic: 19.8 us -> 0 us
  between operations: 13.4 us -> 0.01 us
  local copies, waits for them, and re-layouts: 14.6 us -> 2.81 us
  starting transfers between devices: 9.1 us -> 0 us
    while x14 -> x0, waiting for transfers between devices: 156 us -> none
    all_gather x7 -> x0, blocking collectives: 71.8 us -> none  [layer_part(): lax.all_gather(attended, 'col', axis=0, tiled=True)]
    pallas_call x0 -> x1, Pallas kernels: none -> 69.9 us  [shards(): pl.pallas_call(functools.partial(kernel, (sections, row_count, cols)), ou...]
    while x7 -> x0, blocking collectives: 63 us -> none
    ppermute x7 -> x0, waiting for transfers between devices: 62.5 us -> none  [from_behind(): return lax.ppermute(x, axis, pairs)]
    dot_general x35 -> x0, matrix products: 55 us -> none  [the longest x7 30.4 us: layer_part(): jnp.dot(scaled, proj_weight, preferred_element_type=jnp.float32)]
    psum x7 -> x0, blocking collectives: 37.6 us -> none  [layer_part(): summed = lax.psum(mixed_rows, 'row')]
    ppermute x7 -> x0, starting transfers between devices: 9.04 us -> none  [from_behind(): return lax.ppermute(x, axis, pairs)]
  transfers between devices with their start and end apart: 14 -> 0, of which waited for: 14 -> 0; matrix products, arithmetic and copies ran while one was open for 3% -> 0% of each run, Pallas kernels for 0% -> 0%
where the time goes in v1:
time: 72.9 us; the launch traced here: 72.7 us
  Pallas kernels  69.9 us (96%)
  local copies, waits for them, and re-layouts  2.81 us (4%)
    pallas_call x1, Pallas kernels, shards(): pl.pallas_call(functools.partial(kernel, (sections, row_count, cols)), ou...  69.9 us
    unnamed x2, local copies, waits for them, and re-layouts  2.81 us

profile of v1, /device:TPU:7, one launch (start us, length us, event | category | flops | bytes accessed | tf_op | source)
XLA Modules:
  0.0 72.7 jit_solution(18015955740146827106)
XLA Ops:
  0.0 1.3 %copy.8.lengths = s32[4,2]{1,0:T(4,128)} copy(s32[4,2]{0,1:T(2,128)} %param.13) | data formatting | bytes 64 | tf_op args[6]
  1.3 69.9 %shard_map.73 = bf16[4,8,1024]{2,1,0:T(8,128)(2,1)} custom-call(bf16[4,8,1024]{2,1,0:T(8,128)(2,1)} %hidden.1, bf16[1,1024]{1,0:T(2,128)(2,1)} %gain.1, bf16[1024,3072]{1,0:T(8,128)(2,1)} %bitcast.5, bf16[2048,1024]{1,0:T(8,128)(2,1)} %bitcast.6, bf16[8,512,128]{2,1,0:T(8,128)(2,1)} %bitcast.7, bf16[8,512,128]{2,1,0:T(8,128)(2,1)} %bitcast.8, ...), custom_call_target="tpu_custom_call" | custom-call | tf_op jit(solution)/shard_map/pallas_call | solution.py:370
  71.2 1.5 %copy.10 = bf16[1,4,8,1024]{3,2,1,0:T(8,128)(2,1)} copy(bf16[1,4,8,1024]{3,2,1,0:T(8,128)(2,1)} %bitcast.9) | data formatting | bytes 131072

commit v2 on v1

v2 whole, which is shorter than its diff:
```python
import functools
import math

import jax
import jax.numpy as jnp
from jax import lax
from jax.experimental import pallas as pl
from jax.experimental.pallas import tpu as pltpu
from jax.sharding import PartitionSpec as P

D = 4096
HEADS = 32
KVH = 8
LOTS = 2
MESH = pl.DeviceIdType.MESH


def remainder(values, by):
    if by & (by - 1) == 0:
        return values & (by - 1)
    return lax.rem(values, jnp.full_like(values, by))


def kernel(
    dims,
    hidden,
    gain,
    wq_hbm,
    wo_hbm,
    keys_hbm,
    values_hbm,
    lengths,
    out,
    wq,
    wo,
    keys,
    values,
    state,
    part,
    part_in,
    square,
    square_in,
    q_rows,
    k_rows,
    v_rows,
    a_rows,
    attended,
    gathered,
    mixed,
    arrived,
    load_sem,
    rs_send,
    rs_recv,
    sq_send,
    sq_recv,
    at_send,
    at_recv,
    x_send,
    x_recv,
    y_send,
    y_recv,
):
    sections, row_count, cols = dims
    s = lax.axis_index("section")
    r = lax.axis_index("row")
    c = lax.axis_index("col")
    batch, depth = hidden.shape[1:]
    lots, rows = state.shape[:2]
    micro = rows // batch
    own = rows // cols
    seq_part = batch // cols
    groups, chunk = wq.shape[0], wq.shape[2]
    head_dim = keys.shape[2]
    per = HEADS // KVH
    heads = groups * per
    spots = keys.shape[1]
    pieces, piece = mixed.shape[2], mixed.shape[4]

    def remote(src, dst, send_sem, recv_sem, device):
        return pltpu.make_async_remote_copy(
            src_ref=src,
            dst_ref=dst,
            send_sem=send_sem,
            recv_sem=recv_sem,
            device_id=device,
            device_id_type=MESH,
        )

    loads = [
        pltpu.make_async_copy(
            wq_hbm.at[:, pl.ds(g * chunk, chunk)], wq.at[g], load_sem.at[g]
        )
        for g in range(groups)
    ]
    load_keys = pltpu.make_async_copy(keys_hbm, keys, load_sem.at[groups])
    load_values = pltpu.make_async_copy(values_hbm, values, load_sem.at[groups + 1])
    load_wo = pltpu.make_async_copy(wo_hbm, wo, load_sem.at[groups + 2])
    for load in loads + [load_keys, load_values, load_wo]:
        load.start()

    barrier = pltpu.get_barrier_semaphore()
    greeted = 0
    for k in range(1, cols):
        pl.semaphore_signal(
            barrier, inc=1, device_id=(s, r, lax.rem(c + k, cols)), device_id_type=MESH
        )
        greeted += 1
    for k in range(1, row_count):
        pl.semaphore_signal(
            barrier, inc=1, device_id=(s, lax.rem(r + k, row_count), c), device_id_type=MESH
        )
        greeted += 1
    for step in (1, sections - 1):
        for other in range(row_count):
            pl.semaphore_signal(
                barrier,
                inc=1,
                device_id=(lax.rem(s + step, sections), other, c),
                device_id_type=MESH,
            )
            greeted += 1

    to_row = lax.broadcasted_iota(jnp.int32, (rows, rows), 0)
    from_row = lax.broadcasted_iota(jnp.int32, (rows, rows), 1)
    order = jnp.zeros((rows, rows), jnp.bool_)
    back = jnp.zeros((rows, rows), jnp.bool_)
    for at in range(cols):
        for m in range(micro):
            first, source = at * own + m * seq_part, m * batch + at * seq_part
            inside = (to_row >= first) & (to_row < first + seq_part)
            order = order | (inside & (to_row - from_row == first - source))
            inside = (from_row >= first) & (from_row < first + seq_part)
            back = back | (inside & (from_row - to_row == first - source))
    order = jnp.where(order, 1.0, 0.0).astype(jnp.bfloat16)
    back = jnp.where(back, 1.0, 0.0).astype(jnp.bfloat16)

    row_at = lax.broadcasted_iota(jnp.int32, (own, head_dim), 0)
    lane = lax.broadcasted_iota(jnp.int32, (own, head_dim), 1)
    half = head_dim // 2
    half_lane = jnp.where(lane < half, lane, lane - half).astype(jnp.float32)
    frequency = jnp.exp(half_lane * (-2.0 * math.log(500000.0) / head_dim))
    length_of, cosines, sines = [], [], []
    for lot in range(lots):
        position = jnp.zeros((own, head_dim), jnp.float32)
        length_of.append([])
        for i in range(own):
            length = lengths[i % seq_part, lot * micro + i // seq_part]
            length_of[lot].append(length)
            position = jnp.where(row_at == i, length.astype(jnp.float32), position)
        angles = position * frequency
        cosines.append(jnp.cos(angles))
        sine = jnp.sin(angles)
        sines.append(jnp.where(lane < half, -sine, sine))

    head_at = lax.broadcasted_iota(jnp.int32, (heads, spots), 0)
    spot_at = lax.broadcasted_iota(jnp.int32, (heads, spots), 1)
    head_group = jnp.zeros((heads, spots), jnp.int32)
    for g in range(1, groups):
        head_group = head_group + jnp.where(head_at >= g * per, 1, 0)
    same_group = remainder(spot_at, groups) == head_group

    pl.semaphore_wait(barrier, greeted)

    copies = []
    square_copies, part_copies, attended_copies = [], [], []
    for lot in range(lots):
        @pl.when(s == 0)
        def _():
            entry = hidden[lot * micro : (lot + 1) * micro].astype(jnp.float32)
            entry = entry.reshape(rows, depth).astype(jnp.bfloat16)
            state[lot] = jnp.dot(order, entry, preferred_element_type=jnp.float32)

        @pl.when(s > 0)
        def _():
            for n in range(pieces):
                for other in range(row_count):
                    remote(
                        mixed.at[lot, 0, n],
                        arrived.at[lot, other, n],
                        x_send.at[lot, n, 0],
                        x_recv.at[lot, n, other],
                        (s, r, c),
                    ).wait_recv()
                total = arrived[lot, 0, n]
                for other in range(1, row_count):
                    total = total + arrived[lot, other, n]
                state[lot, :, n * piece : (n + 1) * piece] = total.astype(jnp.bfloat16).astype(
                    jnp.float32
                )

        current = state[lot]
        squares = jnp.sum(current * current, axis=1, keepdims=True)
        squares = jnp.broadcast_to(squares, (rows, head_dim))
        for at in range(cols):
            square[lot, at] = squares[at * own : (at + 1) * own]
        started = []
        for k in range(1, cols):
            peer = lax.rem(c + k, cols)
            started.append(
                remote(
                    square.at[lot, peer],
                    square_in.at[lot, k - 1],
                    sq_send.at[lot, k - 1],
                    sq_recv.at[lot, k - 1],
                    (s, r, peer),
                )
            )
            started[-1].start()
        square_copies.append(started)
        copies += started
        scaled = (current * gain[...].astype(jnp.float32)).astype(jnp.bfloat16)
        part_copies.append([])
        for g in range(groups):
            if lot == 0:
                loads[g].wait()
            product = jnp.dot(scaled, wq[g], preferred_element_type=jnp.float32)
            for at in range(cols):
                part[lot, g, at] = product[at * own : (at + 1) * own]
            started = []
            for k in range(1, cols):
                peer = lax.rem(c + k, cols)
                started.append(
                    remote(
                        part.at[lot, g, peer],
                        part_in.at[lot, g, k - 1],
                        rs_send.at[lot, g, k - 1],
                        rs_recv.at[lot, g, k - 1],
                        (s, r, peer),
                    )
                )
                started[-1].start()
            part_copies[lot].append(started)
            copies += started

    load_keys.wait()
    load_values.wait()
    scale = 1.0 / math.sqrt(head_dim)
    seqs = range(own)
    for lot in range(lots):

        def rotate(vectors):
            return vectors * cosines[lot] + pltpu.roll(vectors, half, 1) * sines[lot]

        for copy in square_copies[lot]:
            copy.wait_recv()
        total = square[lot, c]
        for k in range(1, cols):
            total = total + square_in[lot, k - 1]
        factor = lax.rsqrt(total / D + 1e-05)
        for g in range(groups):
            for copy in part_copies[lot][g]:
                copy.wait_recv()
            total = part[lot, g, c]
            for k in range(1, cols):
                total = total + part_in[lot, g, k - 1]
            cut = [total[:, i * head_dim : (i + 1) * head_dim] * factor for i in range(per + 2)]
            new_key = rotate(cut[per]).astype(jnp.bfloat16).astype(jnp.float32)
            new_value = cut[per + 1].astype(jnp.bfloat16).astype(jnp.float32)
            for i in range(per):
                at = pl.ds((g * per + i) * own, own)
                q_rows[lot, at, :] = rotate(cut[i])
                k_rows[lot, at, :] = new_key
                v_rows[lot, at, :] = new_value
        taken = [pl.ds(i, heads, stride=own) for i in seqs]
        queries = [q_rows[lot, taken[i], :].astype(jnp.bfloat16) for i in seqs]
        scores = [
            lax.dot_general(
                queries[i],
                keys[lot * own + i],
                (((1,), (1,)), ((), ())),
                preferred_element_type=jnp.float32,
            )
            * scale
            for i in seqs
        ]
        own_scores = [
            jnp.sum(
                queries[i].astype(jnp.float32) * k_rows[lot, taken[i], :], axis=1, keepdims=True
            )
            * scale
            for i in seqs
        ]
        weights, own_weights = [], []
        for i in seqs:
            visible = same_group & (spot_at < length_of[lot][i] * groups)
            masked = jnp.where(visible, scores[i], -jnp.inf)
            row_max = jnp.maximum(jnp.max(masked, axis=1, keepdims=True), own_scores[i])
            cache_exp = jnp.exp(masked - row_max)
            own_exp = jnp.exp(own_scores[i] - row_max)
            total = jnp.sum(cache_exp, axis=1, keepdims=True) + own_exp
            weights.append((cache_exp / total).astype(jnp.bfloat16))
            own_weights.append((own_exp / total).astype(jnp.bfloat16).astype(jnp.float32))
        for i in seqs:
            result = jnp.dot(
                weights[i], values[lot * own + i], preferred_element_type=jnp.float32
            )
            a_rows[lot, taken[i], :] = result + own_weights[i] * v_rows[lot, taken[i], :]
        for h in range(heads):
            attended[lot, c, :, h * head_dim : (h + 1) * head_dim] = a_rows[
                lot, h * own : (h + 1) * own, :
            ].astype(jnp.bfloat16)
        started = []
        for k in range(1, cols):
            peer = lax.rem(c + k, cols)
            started.append(
                remote(
                    attended.at[lot, c],
                    attended.at[lot, c],
                    at_send.at[lot, k - 1],
                    at_recv.at[lot, k - 1],
                    (s, r, peer),
                )
            )
            started[-1].start()
        attended_copies.append(started)
        copies += started

    load_wo.wait()

    def onward(lot, n, other):
        return remote(
            mixed.at[lot, r, n],
            arrived.at[lot, r, n],
            x_send.at[lot, n, other],
            x_recv.at[lot, n, r],
            (lax.rem(s + 1, sections), other, c),
        )

    def sideways(lot, n, k):
        return remote(
            mixed.at[lot, r, n],
            mixed.at[lot, r, n],
            y_send.at[lot, n, k - 1],
            y_recv.at[lot, n, k - 1],
            (s, lax.rem(r + k, row_count), c),
        )

    for lot in range(lots):
        for copy in attended_copies[lot]:
            copy.wait_recv()
        for at in range(cols):
            gathered[lot, at * own : (at + 1) * own, :] = attended[lot, at].astype(jnp.float32)
        everyone = gathered[lot].astype(jnp.bfloat16)
        for n in range(pieces):
            at = slice(n * piece, (n + 1) * piece)
            product = jnp.dot(everyone, wo[:, at], preferred_element_type=jnp.float32)
            mixed[lot, r, n] = product + jnp.where(r == 0, state[lot, :, at], 0.0)

            @pl.when(s < sections - 1)
            def _():
                for other in range(row_count):
                    onward(lot, n, other).start()

            @pl.when(s == sections - 1)
            def _():
                for k in range(1, row_count):
                    sideways(lot, n, k).start()

    @pl.when(s < sections - 1)
    def _():
        for lot in range(lots):
            for n in range(pieces):
                for k in range(1, row_count):
                    sideways(lot, n, k).start()

    for lot in range(lots):
        for n in range(pieces):
            for k in range(1, row_count):
                sideways(lot, n, k).wait_recv()
            total = mixed[lot, 0, n]
            for other in range(1, row_count):
                total = total + mixed[lot, other, n]
            final = jnp.dot(back, total.astype(jnp.bfloat16), preferred_element_type=jnp.float32)
            out[lot * micro : (lot + 1) * micro, :, n * piece : (n + 1) * piece] = final.reshape(
                micro, batch, piece
            ).astype(jnp.bfloat16)

    for copy in copies:
        copy.wait_send()
    for lot in range(lots):
        for n in range(pieces):
            for k in range(1, row_count):
                sideways(lot, n, k).wait_send()

    @pl.when(s < sections - 1)
    def _():
        for lot in range(lots):
            for n in range(pieces):
                for other in range(row_count):
                    onward(lot, n, other).wait_send()


def shards(hidden, norm_gain, w_qkv, w_out, cache_keys, cache_values, cache_lengths):
    sections, row_count, cols = (lax.axis_size(a) for a in ("section", "row", "col"))
    micro, batch, depth = hidden.shape
    rows = micro // LOTS * batch
    own = rows // cols
    spots, groups, head_dim = cache_keys.shape[3:]
    per = HEADS // KVH
    heads = groups * per
    chunk = (per + 2) * head_dim
    piece = min(256, w_out.shape[2])
    pieces = w_out.shape[2] // piece
    keys = cache_keys.reshape(LOTS * own, spots * groups, head_dim)
    values = cache_values.reshape(LOTS * own, spots * groups, head_dim)
    vmem = pl.BlockSpec(memory_space=pltpu.VMEM)
    hbm = pl.BlockSpec(memory_space=pl.ANY)
    dma = pltpu.SemaphoreType.DMA
    f32, bf16 = jnp.float32, jnp.bfloat16
    return pl.pallas_call(
        functools.partial(kernel, (sections, row_count, cols)),
        out_shape=jax.ShapeDtypeStruct((micro, batch, depth), bf16),
        in_specs=[vmem, vmem, hbm, hbm, hbm, hbm, pl.BlockSpec(memory_space=pltpu.SMEM)],
        out_specs=vmem,
        scratch_shapes=[
            pltpu.VMEM((groups, depth, chunk), bf16),
            pltpu.VMEM(w_out.shape[1:], bf16),
            pltpu.VMEM(keys.shape, bf16),
            pltpu.VMEM(values.shape, bf16),
            pltpu.VMEM((LOTS, rows, depth), f32),
            pltpu.VMEM((LOTS, groups, cols, own, chunk), f32),
            pltpu.VMEM((LOTS, groups, cols - 1, own, chunk), f32),
            pltpu.VMEM((LOTS, cols, own, head_dim), f32),
            pltpu.VMEM((LOTS, cols - 1, own, head_dim), f32),
            pltpu.VMEM((LOTS, heads * own, head_dim), f32),
            pltpu.VMEM((LOTS, heads * own, head_dim), f32),
            pltpu.VMEM((LOTS, heads * own, head_dim), f32),
            pltpu.VMEM((LOTS, heads * own, head_dim), f32),
            pltpu.VMEM((LOTS, cols, own, heads * head_dim), bf16),
            pltpu.VMEM((LOTS, rows, heads * head_dim), f32),
            pltpu.VMEM((LOTS, row_count, pieces, rows, piece), f32),
            pltpu.VMEM((LOTS, row_count, pieces, rows, piece), f32),
            dma((groups + 3,)),
            dma((LOTS, groups, cols - 1)),
            dma((LOTS, groups, cols - 1)),
            dma((LOTS, cols - 1)),
            dma((LOTS, cols - 1)),
            dma((LOTS, cols - 1)),
            dma((LOTS, cols - 1)),
            dma((LOTS, pieces, row_count)),
            dma((LOTS, pieces, row_count)),
            dma((LOTS, pieces, row_count - 1)),
            dma((LOTS, pieces, row_count - 1)),
        ],
        compiler_params=pltpu.CompilerParams(collective_id=0, has_side_effects=True),
    )(hidden, norm_gain, w_qkv[0], w_out[0], keys, values, cache_lengths.T)[None]


def solution(mesh):
    return jax.shard_map(
        shards,
        mesh=mesh,
        in_specs=(
            P(None, None, "col"),
            P("section", "col"),
            P("section", "col", "row"),
            P("section", "row", "col"),
            P("section", None, "col", None, "row", None),
            P("section", None, "col", None, "row", None),
            P(None, "col"),
        ),
        out_specs=P("section", None, None, "col"),
        check_vma=False,
    )
```

time: 72.9 us -> 61.7 us (0.85)
  Pallas kernels: 69.9 us -> 60 us
  local copies, waits for them, and re-layouts: 2.81 us -> 1.47 us
    pallas_call x1, Pallas kernels: 69.9 us -> 60 us  [shards(): pl.pallas_call(functools.partial(kernel, (sections, row_count, cols)), ou...]
    unnamed x2 -> x1, local copies, waits for them, and re-layouts: 2.81 us -> 1.47 us
where the time goes in v2:
time: 61.7 us; the launch traced here: 61.5 us
  Pallas kernels  60 us (97%)
  local copies, waits for them, and re-layouts  1.47 us (2%)
    pallas_call x1, Pallas kernels, shards(): pl.pallas_call(functools.partial(kernel, (sections, row_count, cols)), ou...  60 us
    unnamed x1, local copies, waits for them, and re-layouts  1.47 us

profile of v2, /device:TPU:7, one launch (start us, length us, event | category | flops | bytes accessed | tf_op | source)
XLA Modules:
  0.0 61.5 jit_solution(12681737916686462230)
XLA Ops:
  0.0 60.0 %shard_map.73 = bf16[4,8,1024]{2,1,0:T(8,128)(2,1)} custom-call(bf16[4,8,1024]{2,1,0:T(8,128)(2,1)} %hidden.1, bf16[1,1024]{1,0:T(2,128)(2,1)} %gain.1, bf16[1024,3072]{1,0:T(8,128)(2,1)} %bitcast.6, bf16[2048,1024]{1,0:T(8,128)(2,1)} %bitcast.7, bf16[8,512,128]{2,1,0:T(8,128)(2,1)} %bitcast.8, bf16[8,512,128]{2,1,0:T(8,128)(2,1)} %bitcast.9, s32[2,4]{1,0:T(2,128)} %bitcast.11), custom_call_target="tpu_custom_call" | custom-call | tf_op jit(solution)/shard_map/pallas_call | solution.py:410
  60.0 1.5 %copy.9 = bf16[1,4,8,1024]{3,2,1,0:T(8,128)(2,1)} copy(bf16[1,4,8,1024]{3,2,1,0:T(8,128)(2,1)} %bitcast.10) | data formatting | bytes 131072

commit v3 on v2

--- a/solution.py
+++ b/solution.py
@@ -11,7 +11,7 @@
 D = 4096
 HEADS = 32
 KVH = 8
-LOTS = 2
+LOTS = 4
 MESH = pl.DeviceIdType.MESH
 
 

time: 61.7 us -> 73 us (1.18)
  Pallas kernels: 60 us -> 70.8 us
    pallas_call x1, Pallas kernels: 60 us -> 70.8 us  [shards(): pl.pallas_call(functools.partial(kernel, (sections, row_count, cols)), ou...]
where the time goes in v3:
time: 73 us; the launch traced here: 72.2 us
  Pallas kernels  70.8 us (97%)
  local copies, waits for them, and re-layouts  1.47 us (2%)
    pallas_call x1, Pallas kernels, shards(): pl.pallas_call(functools.partial(kernel, (sections, row_count, cols)), ou...  70.8 us
    unnamed x1, local copies, waits for them, and re-layouts  1.47 us

profile of v3, /device:TPU:7, one launch (start us, length us, event | category | flops | bytes accessed | tf_op | source)
XLA Modules:
  0.0 72.2 jit_solution(5820317286778346442)
XLA Ops:
  0.0 70.8 %shard_map.73 = bf16[4,8,1024]{2,1,0:T(8,128)(2,1)} custom-call(bf16[4,8,1024]{2,1,0:T(8,128)(2,1)} %hidden.1, bf16[1,1024]{1,0:T(2,128)(2,1)} %gain.1, bf16[1024,3072]{1,0:T(8,128)(2,1)} %bitcast.6, bf16[2048,1024]{1,0:T(8,128)(2,1)} %bitcast.7, bf16[8,512,128]{2,1,0:T(8,128)(2,1)} %bitcast.8, bf16[8,512,128]{2,1,0:T(8,128)(2,1)} %bitcast.9, s32[2,4]{1,0:T(2,128)} %bitcast.11), custom_call_target="tpu_custom_call" | custom-call | tf_op jit(solution)/shard_map/pallas_call | solution.py:410
  70.8 1.5 %copy.9 = bf16[1,4,8,1024]{3,2,1,0:T(8,128)(2,1)} copy(bf16[1,4,8,1024]{3,2,1,0:T(8,128)(2,1)} %bitcast.10) | data formatting | bytes 131072

commit v4 on v2

--- a/solution.py
+++ b/solution.py
@@ -12,6 +12,8 @@
 HEADS = 32
 KVH = 8
 LOTS = 2
+CUTS = 4
+PIECE = 512
 MESH = pl.DeviceIdType.MESH
 
 
@@ -23,14 +25,17 @@
 
 def kernel(
     dims,
-    hidden,
-    gain,
+    hidden_hbm,
+    gain_hbm,
     wq_hbm,
     wo_hbm,
     keys_hbm,
     values_hbm,
+    lengths_hbm,
+    out,
+    hidden,
+    gain,
     lengths,
-    out,
     wq,
     wo,
     keys,
@@ -38,8 +43,6 @@
     state,
     part,
     part_in,
-    square,
-    square_in,
     q_rows,
     k_rows,
     v_rows,
@@ -51,8 +54,6 @@
     load_sem,
     rs_send,
     rs_recv,
-    sq_send,
-    sq_recv,
     at_send,
     at_recv,
     x_send,
@@ -75,6 +76,9 @@
     heads = groups * per
     spots = keys.shape[1]
     pieces, piece = mixed.shape[2], mixed.shape[4]
+    cuts = part.shape[1]
+    grouped = groups // cuts
+    width = grouped * chunk
 
     def remote(src, dst, send_sem, recv_sem, device):
         return pltpu.make_async_remote_copy(
@@ -95,7 +99,10 @@
     load_keys = pltpu.make_async_copy(keys_hbm, keys, load_sem.at[groups])
     load_values = pltpu.make_async_copy(values_hbm, values, load_sem.at[groups + 1])
     load_wo = pltpu.make_async_copy(wo_hbm, wo, load_sem.at[groups + 2])
-    for load in loads + [load_keys, load_values, load_wo]:
+    load_lengths = pltpu.make_async_copy(lengths_hbm, lengths, load_sem.at[groups + 3])
+    load_hidden = pltpu.make_async_copy(hidden_hbm, hidden, load_sem.at[groups + 4])
+    load_gain = pltpu.make_async_copy(gain_hbm, gain, load_sem.at[groups + 5])
+    for load in [load_lengths, load_hidden, load_gain] + loads + [load_keys, load_values, load_wo]:
         load.start()
 
     barrier = pltpu.get_barrier_semaphore()
@@ -139,6 +146,7 @@
     half = head_dim // 2
     half_lane = jnp.where(lane < half, lane, lane - half).astype(jnp.float32)
     frequency = jnp.exp(half_lane * (-2.0 * math.log(500000.0) / head_dim))
+    load_lengths.wait()
     length_of, cosines, sines = [], [], []
     for lot in range(lots):
         position = jnp.zeros((own, head_dim), jnp.float32)
@@ -159,17 +167,21 @@
         head_group = head_group + jnp.where(head_at >= g * per, 1, 0)
     same_group = remainder(spot_at, groups) == head_group
 
-    pl.semaphore_wait(barrier, greeted)
-
-    copies = []
-    square_copies, part_copies, attended_copies = [], [], []
-    for lot in range(lots):
-        @pl.when(s == 0)
-        def _():
+    load_hidden.wait()
+    load_gain.wait()
+
+    @pl.when(s == 0)
+    def _():
+        for lot in range(lots):
             entry = hidden[lot * micro : (lot + 1) * micro].astype(jnp.float32)
             entry = entry.reshape(rows, depth).astype(jnp.bfloat16)
             state[lot] = jnp.dot(order, entry, preferred_element_type=jnp.float32)
 
+    pl.semaphore_wait(barrier, greeted)
+
+    copies = []
+    part_copies, attended_copies = [], []
+    for lot in range(lots):
         @pl.when(s > 0)
         def _():
             for n in range(pieces):
@@ -192,39 +204,30 @@
         squares = jnp.sum(current * current, axis=1, keepdims=True)
         squares = jnp.broadcast_to(squares, (rows, head_dim))
         for at in range(cols):
-            square[lot, at] = squares[at * own : (at + 1) * own]
-        started = []
-        for k in range(1, cols):
-            peer = lax.rem(c + k, cols)
-            started.append(
-                remote(
-                    square.at[lot, peer],
-                    square_in.at[lot, k - 1],
-                    sq_send.at[lot, k - 1],
-                    sq_recv.at[lot, k - 1],
-                    (s, r, peer),
-                )
-            )
-            started[-1].start()
-        square_copies.append(started)
-        copies += started
+            part[lot, 0, at, :, width:] = squares[at * own : (at + 1) * own]
         scaled = (current * gain[...].astype(jnp.float32)).astype(jnp.bfloat16)
         part_copies.append([])
         for g in range(groups):
             if lot == 0:
                 loads[g].wait()
             product = jnp.dot(scaled, wq[g], preferred_element_type=jnp.float32)
+            cut, at_lane = g // grouped, g % grouped * chunk
             for at in range(cols):
-                part[lot, g, at] = product[at * own : (at + 1) * own]
+                part[lot, cut, at, :, at_lane : at_lane + chunk] = product[
+                    at * own : (at + 1) * own
+                ]
+            if (g + 1) % grouped:
+                continue
             started = []
+            sent = pl.ds(0, width + head_dim if cut == 0 else width)
             for k in range(1, cols):
                 peer = lax.rem(c + k, cols)
                 started.append(
                     remote(
-                        part.at[lot, g, peer],
-                        part_in.at[lot, g, k - 1],
-                        rs_send.at[lot, g, k - 1],
-                        rs_recv.at[lot, g, k - 1],
+                        part.at[lot, cut, peer, :, sent],
+                        part_in.at[lot, cut, k - 1, :, sent],
+                        rs_send.at[lot, cut, k - 1],
+                        rs_recv.at[lot, cut, k - 1],
                         (s, r, peer),
                     )
                 )
@@ -241,18 +244,19 @@
         def rotate(vectors):
             return vectors * cosines[lot] + pltpu.roll(vectors, half, 1) * sines[lot]
 
-        for copy in square_copies[lot]:
-            copy.wait_recv()
-        total = square[lot, c]
-        for k in range(1, cols):
-            total = total + square_in[lot, k - 1]
-        factor = lax.rsqrt(total / D + 1e-05)
         for g in range(groups):
-            for copy in part_copies[lot][g]:
-                copy.wait_recv()
-            total = part[lot, g, c]
+            cut, lanes = g // grouped, slice(g % grouped * chunk, (g % grouped + 1) * chunk)
+            if g % grouped == 0:
+                for copy in part_copies[lot][cut]:
+                    copy.wait_recv()
+            if g == 0:
+                total = part[lot, 0, c, :, width:]
+                for k in range(1, cols):
+                    total = total + part_in[lot, 0, k - 1, :, width:]
+                factor = lax.rsqrt(total / D + 1e-05)
+            total = part[lot, cut, c, :, lanes]
             for k in range(1, cols):
-                total = total + part_in[lot, g, k - 1]
+                total = total + part_in[lot, cut, k - 1, :, lanes]
             cut = [total[:, i * head_dim : (i + 1) * head_dim] * factor for i in range(per + 2)]
             new_key = rotate(cut[per]).astype(jnp.bfloat16).astype(jnp.float32)
             new_value = cut[per + 1].astype(jnp.bfloat16).astype(jnp.float32)
@@ -399,7 +403,9 @@
     per = HEADS // KVH
     heads = groups * per
     chunk = (per + 2) * head_dim
-    piece = min(256, w_out.shape[2])
+    piece = min(PIECE, w_out.shape[2])
+    cuts = min(CUTS, groups)
+    width = groups // cuts * chunk + head_dim
     pieces = w_out.shape[2] // piece
     keys = cache_keys.reshape(LOTS * own, spots * groups, head_dim)
     values = cache_values.reshape(LOTS * own, spots * groups, head_dim)
@@ -409,19 +415,20 @@
     f32, bf16 = jnp.float32, jnp.bfloat16
     return pl.pallas_call(
         functools.partial(kernel, (sections, row_count, cols)),
-        out_shape=jax.ShapeDtypeStruct((micro, batch, depth), bf16),
-        in_specs=[vmem, vmem, hbm, hbm, hbm, hbm, pl.BlockSpec(memory_space=pltpu.SMEM)],
+        out_shape=pltpu.VMEM((micro, batch, depth), bf16),
+        in_specs=[hbm] * 7,
         out_specs=vmem,
         scratch_shapes=[
+            pltpu.VMEM(hidden.shape, bf16),
+            pltpu.VMEM(norm_gain.shape, bf16),
+            pltpu.SMEM(cache_lengths.T.shape, jnp.int32),
             pltpu.VMEM((groups, depth, chunk), bf16),
             pltpu.VMEM(w_out.shape[1:], bf16),
             pltpu.VMEM(keys.shape, bf16),
             pltpu.VMEM(values.shape, bf16),
             pltpu.VMEM((LOTS, rows, depth), f32),
-            pltpu.VMEM((LOTS, groups, cols, own, chunk), f32),
-            pltpu.VMEM((LOTS, groups, cols - 1, own, chunk), f32),
-            pltpu.VMEM((LOTS, cols, own, head_dim), f32),
-            pltpu.VMEM((LOTS, cols - 1, own, head_dim), f32),
+            pltpu.VMEM((LOTS, cuts, cols, own, width), f32),
+            pltpu.VMEM((LOTS, cuts, cols - 1, own, width), f32),
             pltpu.VMEM((LOTS, heads * own, head_dim), f32),
             pltpu.VMEM((LOTS, heads * own, head_dim), f32),
             pltpu.VMEM((LOTS, heads * own, head_dim), f32),
@@ -430,11 +437,9 @@
             pltpu.VMEM((LOTS, rows, heads * head_dim), f32),
             pltpu.VMEM((LOTS, row_count, pieces, rows, piece), f32),
             pltpu.VMEM((LOTS, row_count, pieces, rows, piece), f32),
-            dma((groups + 3,)),
-            dma((LOTS, groups, cols - 1)),
-            dma((LOTS, groups, cols - 1)),
-            dma((LOTS, cols - 1)),
-            dma((LOTS, cols - 1)),
+            dma((groups + 6,)),
+            dma((LOTS, cuts, cols - 1)),
+            dma((LOTS, cuts, cols - 1)),
             dma((LOTS, cols - 1)),
             dma((LOTS, cols - 1)),
             dma((LOTS, pieces, row_count)),

time: 61.7 us -> 57.1 us (0.925)
  Pallas kernels: 60 us -> 56.3 us
  local copies, waits for them, and re-layouts: 1.47 us -> 0.63 us
    pallas_call x1, Pallas kernels: 60 us -> 56.3 us  [shards(): pl.pallas_call(functools.partial(kernel, (sections, row_count, cols)), ou...]
    unnamed x1, local copies, waits for them, and re-layouts: 1.47 us -> 0.63 us
where the time goes in v4:
time: 57.1 us; the launch traced here: 57 us
  Pallas kernels  56.3 us (99%)
  local copies, waits for them, and re-layouts  0.63 us (1%)
    pallas_call x1, Pallas kernels, shards(): pl.pallas_call(functools.partial(kernel, (sections, row_count, cols)), ou...  56.3 us

profile of v4, /device:TPU:7, one launch (start us, length us, event | category | flops | bytes accessed | tf_op | source)
XLA Modules:
  0.0 57.0 jit_solution(17915252342144951230)
XLA Ops:
  0.0 56.3 %shard_map.73 = bf16[4,8,1024]{2,1,0:T(8,128)(2,1)S(1)} custom-call(bf16[4,8,1024]{2,1,0:T(8,128)(2,1)} %hidden_hbm.1, bf16[1,1024]{1,0:T(2,128)(2,1)} %gain_hbm.1, bf16[1024,3072]{1,0:T(8,128)(2,1)} %bitcast.7, bf16[2048,1024]{1,0:T(8,128)(2,1)} %bitcast.8, bf16[8,512,128]{2,1,0:T(8,128)(2,1)} %bitcast.9, bf16[8,512,128]{2,1,0:T(8,128)(2,1)} %bitcast.10, ...), custom_call_target="tpu_custom_call" | custom-call | tf_op jit(solution)/shard_map/pallas_call | solution.py:416
  56.3 0.6 %copy.9 = bf16[1,4,8,1024]{3,2,1,0:T(8,128)(2,1)} copy(bf16[1,4,8,1024]{3,2,1,0:T(8,128)(2,1)S(1)} %bitcast.6) | data formatting | bytes 131072

commit v5 on v4

--- a/solution.py
+++ b/solution.py
@@ -11,9 +11,9 @@
 D = 4096
 HEADS = 32
 KVH = 8
-LOTS = 2
-CUTS = 4
-PIECE = 512
+LOTS = 4
+CUTS = 2
+PIECE = 1024
 MESH = pl.DeviceIdType.MESH
 
 
@@ -105,11 +105,19 @@
     for load in [load_lengths, load_hidden, load_gain] + loads + [load_keys, load_values, load_wo]:
         load.start()
 
+    if cols % 2 == 0:
+        peers = [
+            lax.rem(k - c + cols, cols) if k % 2 else lax.rem(c + k, cols)
+            for k in range(cols - 1, 0, -1)
+        ]
+    else:
+        peers = [lax.rem(c + k, cols) for k in range(1, cols)]
+
     barrier = pltpu.get_barrier_semaphore()
     greeted = 0
     for k in range(1, cols):
         pl.semaphore_signal(
-            barrier, inc=1, device_id=(s, r, lax.rem(c + k, cols)), device_id_type=MESH
+            barrier, inc=1, device_id=(s, r, peers[k - 1]), device_id_type=MESH
         )
         greeted += 1
     for k in range(1, row_count):
@@ -221,7 +229,7 @@
             started = []
             sent = pl.ds(0, width + head_dim if cut == 0 else width)
             for k in range(1, cols):
-                peer = lax.rem(c + k, cols)
+                peer = peers[k - 1]
                 started.append(
                     remote(
                         part.at[lot, cut, peer, :, sent],
@@ -305,7 +313,7 @@
             ].astype(jnp.bfloat16)
         started = []
         for k in range(1, cols):
-            peer = lax.rem(c + k, cols)
+            peer = peers[k - 1]
             started.append(
                 remote(
                     attended.at[lot, c],
@@ -327,7 +335,7 @@
             arrived.at[lot, r, n],
             x_send.at[lot, n, other],
             x_recv.at[lot, n, r],
-            (lax.rem(s + 1, sections), other, c),
+            (lax.rem(s + 1, sections), lax.rem(r + 1 + other, row_count), c),
         )
 
     def sideways(lot, n, k):

time: 57.1 us -> 55.8 us (0.977)
  Pallas kernels: 56.3 us -> 54.6 us
    pallas_call x1, Pallas kernels: 56.3 us -> 54.6 us  [shards(): pl.pallas_call(functools.partial(kernel, (sections, row_count, cols)), ou...]
where the time goes in v5:
time: 55.8 us; the launch traced here: 55.2 us
  Pallas kernels  54.6 us (98%)
  local copies, waits for them, and re-layouts  0.63 us (1%)
    pallas_call x1, Pallas kernels, shards(): pl.pallas_call(functools.partial(kernel, (sections, row_count, cols)), ou...  54.6 us

profile of v5, /device:TPU:7, one launch (start us, length us, event | category | flops | bytes accessed | tf_op | source)
XLA Modules:
  0.0 55.2 jit_solution(6258847368111993921)
XLA Ops:
  0.0 54.6 %shard_map.73 = bf16[4,8,1024]{2,1,0:T(8,128)(2,1)S(1)} custom-call(bf16[4,8,1024]{2,1,0:T(8,128)(2,1)} %hidden_hbm.1, bf16[1,1024]{1,0:T(2,128)(2,1)} %gain_hbm.1, bf16[1024,3072]{1,0:T(8,128)(2,1)} %bitcast.7, bf16[2048,1024]{1,0:T(8,128)(2,1)} %bitcast.8, bf16[8,512,128]{2,1,0:T(8,128)(2,1)} %bitcast.9, bf16[8,512,128]{2,1,0:T(8,128)(2,1)} %bitcast.10, ...), custom_call_target="tpu_custom_call" | custom-call | tf_op jit(solution)/shard_map/pallas_call | solution.py:424
  54.6 0.6 %copy.9 = bf16[1,4,8,1024]{3,2,1,0:T(8,128)(2,1)} copy(bf16[1,4,8,1024]{3,2,1,0:T(8,128)(2,1)S(1)} %bitcast.6) | data formatting | bytes 131072
